TPU v7x, 256 devices: a whole 4x4x8 slice. The times are simulated.
256 devices in a mesh: hist: 32 (over x, z_hi, y), row: 4 (over z_lo), cur: 2 (over core).
Axes of the slice: x: 4, y: 4, z: 8 (z_hi: 2, z_lo: 4; z = z_hi * 4 + z_lo), core: 2. Of those that a mesh axis runs over, the one named last changes fastest.
Arguments:
- incident: bfloat16 [4, 256, 256, 64], P(None, ('hist', 'row', 'cur')), may hold values from -6 to 6
- past: bfloat16 [256, 8, 256, 64], P(('hist', 'row', 'cur')), may hold values from -6 to 6
- hist_tiles: bfloat16 [256, 64, 256, 256], P(('hist', 'row', 'cur')), may hold values from -0.046875 to 0.046875
- tile_rows: int32 [256, 64], P(('hist', 'row', 'cur')), may hold values from 0 to 31
- tile_cols: int32 [256, 64], P(('hist', 'row', 'cur')), may hold values from 0 to 7
- tile_lags: int32 [256, 64], P(('hist', 'row', 'cur')), may hold values from 4 to 8
- tile_scales: float32 [256, 64], P(('hist', 'row', 'cur')), may hold values from 0.5 to 2
- near_tiles: bfloat16 [256, 3, 5, 256, 256], P(('hist', 'row', 'cur')), may hold values from -0.09375 to 0.09375
- inverses: bfloat16 [256, 256, 256], P(('hist', 'row', 'cur')), may hold values from -0.21875 to 0.21875
Outputs:
- densities: bfloat16 [4, 256, 256, 64], P(None, ('hist', 'row', 'cur'))
All inputs are finite; a program needn't handle non-finite values.
Results may differ from a plain program's by a relative error of at most 0.02.
Values may be sent and summed in bfloat16 or wider, within the bound.
A program may use at most 128 MiB of HBM per device.

v0:
```python
import jax
import jax.numpy as jnp
from jax import lax
from jax.sharding import Mesh
from jax.sharding import PartitionSpec as P

HIST_ROW_CUR = ("hist_0", "hist_1", "hist_2", "row", "cur")
HIST = ("hist_0", "hist_1", "hist_2")


def shifted(block, axis, distance):
    devices = range(lax.axis_size(axis))
    route = [(i - distance, i) for i in devices if i - distance in devices]
    return lax.ppermute(block, axis, route)


def sent_to_all(value, axis):
    size = lax.axis_size(axis)
    return lax.all_to_all(
        jnp.broadcast_to(value[None], (size, *value.shape)), axis, 0, 0, tiled=True
    )


def in_order(blocks, dim):
    shape = list(blocks.shape[1:])
    shape[dim] *= blocks.shape[0]
    return jnp.moveaxis(blocks, 0, dim).reshape(shape)


def gathered_copies(value, axis, dim):
    blocks = sent_to_all(value, axis)
    return in_order(blocks, dim)


def sum_in_order(blocks, axes, sequence):
    shape = [lax.axis_size(a) for a in axes]
    blocks = blocks.reshape(*shape, *blocks.shape[1:])
    blocks = blocks.transpose(*sequence, *range(len(axes), blocks.ndim))
    blocks = blocks.reshape(-1, *blocks.shape[len(axes) :])
    for k in sequence:
        blocks = lax.psum_scatter(blocks, axes[k], scatter_dimension=0, tiled=True)
    return blocks[0]


def split_up(value, dim, size):
    shape = value.shape
    blocks = value.reshape(*shape[:dim], size, shape[dim] // size, *shape[dim + 1 :])
    return jnp.moveaxis(blocks, dim, 0)


def sum_by_axis(value, axes, sequence, dim):
    size = lax.axis_size(axes)
    return sum_in_order(split_up(value, dim, size), axes, sequence)


def start_cycle(window):
    pieces = []
    for amount in (2, 1, 0, -1, -2):
        if amount == 0:
            pieces.append(window)
        else:
            pieces.append(shifted(window, HIST_ROW_CUR, amount))
    return jnp.stack(pieces)


def newest_cycle(fresh):
    pieces = []
    for amount in (2, 1, 0, -1, -2):
        if amount == 0:
            pieces.append(fresh)
        else:
            pieces.append(shifted(fresh, HIST_ROW_CUR, amount))
    return jnp.stack(pieces)


def on_device(
    incident, past, hist_tiles, tile_rows, tile_cols, tile_lags, tile_scales, near_tiles, inverses
):
    step_count = incident.shape[0]
    kept = past.shape[1]
    group_past = gathered_copies(past, ("row", "cur"), 0)
    when = jnp.arange(step_count, dtype=jnp.int32)[:, None] - tile_lags[0][None, :] + kept
    picked = group_past[tile_cols[0][None, :], when]
    terms = jnp.einsum("kij,skjr->skir", hist_tiles[0], picked, preferred_element_type=jnp.float32)
    terms = terms * tile_scales[0][None, :, None, None]
    terms_high = terms.astype(jnp.bfloat16)
    terms_low = (terms - terms_high.astype(jnp.float32)).astype(jnp.bfloat16)
    targets = tile_rows[0]
    owners = jnp.arange(lax.axis_size(HIST), dtype=jnp.int32)
    onehot = (targets[None, :] == owners[:, None]).astype(jnp.bfloat16)
    upper = jnp.einsum("gk,skir->gsir", onehot, terms_high, preferred_element_type=jnp.float32)
    lower = jnp.einsum("gk,skir->gsir", onehot, terms_low, preferred_element_type=jnp.float32)
    history = sum_by_axis((upper + lower).astype(jnp.bfloat16), HIST, (0, 2, 1), 0).astype(
        jnp.float32
    )
    window = past[0, kept - 3 :]
    cycle = start_cycle(window)
    made = []
    for step in range(step_count):
        arranged = jnp.swapaxes(cycle[:, ::-1], 0, 1)
        near = jnp.einsum(
            "loij,lojr->ir", near_tiles[0], arranged, preferred_element_type=jnp.float32
        )
        rhs = (incident[step, 0].astype(jnp.float32) - history[0, step] - near).astype(jnp.bfloat16)
        fresh = jnp.dot(inverses[0], rhs, preferred_element_type=jnp.float32).astype(jnp.bfloat16)
        made.append(fresh)
        if step + 1 < step_count:
            spread = newest_cycle(fresh)
            cycle = jnp.concatenate([cycle[:, 1:], spread[:, None]], axis=1)
    return jnp.stack(made)[:, None]


def solution(mesh):
    torus = Mesh(
        mesh.devices.reshape(4, 2, 4, mesh.shape["row"], mesh.shape["cur"]),
        ("hist_0", "hist_1", "hist_2", "row", "cur"),
    )
    placed = (
        P(None, HIST_ROW_CUR, None, None),
        P(HIST_ROW_CUR, None, None, None),
        P(HIST_ROW_CUR, None, None, None),
        P(HIST_ROW_CUR, None),
        P(HIST_ROW_CUR, None),
        P(HIST_ROW_CUR, None),
        P(HIST_ROW_CUR, None),
        P(HIST_ROW_CUR, None, None, None, None),
        P(HIST_ROW_CUR, None, None),
    )
    return jax.shard_map(
        on_device,
        mesh=torus,
        in_specs=placed,
        out_specs=P(None, HIST_ROW_CUR, None, None),
        check_vma=False,
    )
```

profile of v0, /device:TPU:3, one launch (start us, length us, event | category | flops | bytes accessed | tf_op | source)
XLA Modules:
  0.0 312.9 jit_solution(888010990463760833)
XLA Ops:
  6.5 2.6 broadcast_in_dim.31
  9.2 6.6 %all-to-all-start = ((bf16[8,1,8,256,64]{3,4,2,1,0:T(8,128)(2,1)}), bf16[8,1,8,256,64]{3,4,2,1,0:T(8,128)(2,1)}, u32[]{:S(2)}, u32[]{:S(2)}) async-start(bf16[8,1,8,256,64]{3,4,2,1,0:T(8,128)(2,1)} %broadcast_in_dim.31), calls=%async_computation | async-start | bytes 4194304 | tf_op jit(solution)/shard_map/all_to_all | solution.py:19
  15.8 0.7 fusion.103
  16.4 0.7 fusion.100
  17.1 0.1 reshape.89
  17.2 46.8 %all-to-all-done = bf16[8,1,8,256,64]{3,4,2,1,0:T(8,128)(2,1)} async-done(((bf16[8,1,8,256,64]{3,4,2,1,0:T(8,128)(2,1)}), bf16[8,1,8,256,64]{3,4,2,1,0:T(8,128)(2,1)}, u32[]{:S(2)}, u32[]{:S(2)}) %all-to-all-start) | async-done | bytes 2097184 | tf_op jit(solution)/shard_map/all_to_all | solution.py:19
  63.9 11.7 %gather_fusion = bf16[256,256,64]{1,2,0:T(8,128)(2,1)} fusion(bf16[8,8,256,64]{2,3,1,0:T(8,128)(2,1)} %bitcast.4, s32[256]{0:T(256)S(1)} %reshape.89), kind=kCustom, calls=%fused_computation | custom fusion | bytes 16779264 | tf_op jit(solution)/shard_map/gather | solution.py:83
  75.7 15.9 %fusion = (bf16[4,64,256,64]{2,3,0,1:T(8,128)(2,1)}, f32[64,4,64,256]{3,2,1,0:T(8,128)}) fusion(f32[64]{0:T(128)S(1)} %bitcast.243, bf16[1,64,256,256]{3,2,1,0:T(8,128)(2,1)} %param.11, bf16[4,64,256,64]{2,3,1,0:T(8,128)(2,1)} %bitcast.229), kind=kOutput, calls=%fused_computation.3 | convolution fusion | flops 2168455168 | bytes 41943296 | tf_op jit(solution)/shard_map/kij,skjr->skir/dot_general | solution.py:84
  91.6 7.9 %bitcast_convert_fusion = bf16[4,64,256,64]{2,3,0,1:T(8,128)(2,1)S(1)} fusion(f32[64,4,64,256]{3,2,1,0:T(8,128)} %get-tuple-element.6, f32[64]{0:T(128)S(1)} %bitcast.244), kind=kLoop, calls=%fused_computation.2 | loop fusion | flops 8388608 | bytes 25166080 | tf_op jit(solution)/shard_map/convert_element_type | solution.py:86
  99.5 0.3 copy-done.1
  99.8 6.0 %fusion.3 = f32[32,4,256,64]{2,0,3,1:T(8,128)S(1)} fusion(bf16[4,64,256,64]{2,3,0,1:T(8,128)(2,1)S(1)} %copy-done.1, s32[64]{0:T(128)S(1)} %bitcast.245), kind=kOutput, calls=%fused_computation.6 | convolution fusion | flops 268437504 | bytes 16777472 | tf_op jit(solution)/shard_map/gk,skir->gsir/dot_general | solution.py:92
  105.8 7.8 %add_convert_fusion = bf16[32,4,256,64]{2,0,3,1:T(8,128)(2,1)} fusion(f32[32,4,256,64]{2,0,3,1:T(8,128)S(1)} %fusion.3, bf16[4,64,256,64]{2,3,0,1:T(8,128)(2,1)S(1)} %bitcast_convert_fusion, s32[64]{0:T(128)S(1)} %bitcast.246), kind=kOutput, calls=%fused_computation.11 | convolution fusion | flops 272631808 | bytes 20971776 | tf_op jit(solution)/shard_map/gk,skir->gsir/dot_general | solution.py:91
  113.6 6.9 %reshape_reshape.3 = bf16[4,2,4,1,4,256,64]{5,2,1,0,6,4,3:T(4,128)(2,1)} reshape(bf16[32,4,256,64]{2,0,3,1:T(8,128)(2,1)} %add_convert_fusion) | data formatting | bytes 8388608 | tf_op jit(solution)/shard_map/reshape;reshape | solution.py:37
  120.5 6.6 %copy.42 = bf16[4,4,2,1,4,256,64]{5,6,4,2,1,0,3:T(8,128)(2,1)} copy(bf16[4,4,2,1,4,256,64]{5,1,2,0,6,4,3:T(4,128)(2,1)} %bitcast.231) | data formatting | bytes 8388608 | tf_op jit(solution)/shard_map/transpose | solution.py:38
  127.2 49.8 %reduce-scatter.4.cloned.1.call-done = bf16[8,1,4,256,64]{3,4,2,1,0:T(8,128)(2,1)} async-done(((bf16[32,1,4,256,64]{3,4,2,1,0:T(8,128)(2,1)}), bf16[8,1,4,256,64]{3,4,2,1,0:T(8,128)(2,1)}) %reduce-scatter.4.cloned.1.call-update) | async-done | bytes 1048592 | tf_op jit(solution)/shard_map/reduce_scatter | solution.py:41
  177.1 3.2 %collective-permute-start = (bf16[3,256,64]{1,2,0:T(8,128)(2,1)S(1)}, bf16[3,256,64]{1,2,0:T(8,128)(2,1)S(1)}, u32[]{:S(2)}, u32[]{:S(2)}) collective-permute-start(bf16[3,256,64]{1,2,0:T(8,128)(2,1)S(1)} %slice_bitcast_fusion), channel_id=1, source_target_pairs={{0,2},{1,3},{2,4},{3,5},{4,6},{5,7},{6,8},{7,9},{8,10},{9,11},{10,... | collective-permute-start | bytes 294920 | tf_op jit(solution)/shard_map/ppermute | solution.py:14
  180.2 7.1 %collective-permute-start.3 = (bf16[3,256,64]{1,2,0:T(8,128)(2,1)S(1)}, bf16[3,256,64]{1,2,0:T(8,128)(2,1)S(1)}, u32[]{:S(2)}, u32[]{:S(2)}) collective-permute-start(bf16[3,256,64]{1,2,0:T(8,128)(2,1)S(1)} %slice_bitcast_fusion), channel_id=1, source_target_pairs={{2,0},{3,1},{4,2},{5,3},{6,4},{7,5},{8,6},{9,7},{10,8},{11,9},{12,... | collective-permute-start | bytes 294920 | tf_op jit(solution)/shard_map/ppermute | solution.py:14
  187.3 2.9 collective-permute-start.2
  190.3 2.6 collective-permute-start.1
  192.9 1.6 collective-permute-done.1
  194.6 10.9 %reduce-scatter.6.cloned.1.call-done = bf16[2,1,4,256,64]{3,4,2,1,0:T(8,128)(2,1)} async-done(((bf16[8,1,4,256,64]{3,4,2,1,0:T(8,128)(2,1)}), bf16[2,1,4,256,64]{3,4,2,1,0:T(8,128)(2,1)}) %reduce-scatter.6.cloned.1.call-update) | async-done | bytes 262160 | tf_op jit(solution)/shard_map/reduce_scatter | solution.py:41
  205.6 25.8 %reduce-scatter.8.cloned.1.call-done = bf16[1,1,4,256,64]{3,4,2,1,0:T(8,128)(2,1)} async-done(((bf16[2,1,4,256,64]{3,4,2,1,0:T(8,128)(2,1)}), bf16[1,1,4,256,64]{3,4,2,1,0:T(8,128)(2,1)}) %reduce-scatter.8.cloned.1.call-update) | async-done | bytes 131088 | tf_op jit(solution)/shard_map/reduce_scatter | solution.py:41
  231.4 0.9 bitcast_convert_fusion.1
  232.3 1.6 convolution_convert_fusion.3
  233.9 5.1 %collective-permute-start.4 = (bf16[256,64]{0,1:T(8,128)(2,1)S(1)}, bf16[256,64]{0,1:T(8,128)(2,1)S(1)}, u32[]{:S(2)}, u32[]{:S(2)}) collective-permute-start(bf16[256,64]{0,1:T(8,128)(2,1)S(1)} %bitcast.237), channel_id=1, source_target_pairs={{0,2},{1,3},{2,4},{3,5},{4,6},{5,7},{6,8},{7,9},{8,10},{9,11},{10,... | collective-permute-start | bytes 98312 | tf_op jit(solution)/shard_map/ppermute | solution.py:14
  239.1 2.9 collective-permute-start.6
  242.0 2.7 collective-permute-start.5
  244.6 8.6 %collective-permute-start.7 = (bf16[256,64]{0,1:T(8,128)(2,1)S(1)}, bf16[256,64]{0,1:T(8,128)(2,1)S(1)}, u32[]{:S(2)}, u32[]{:S(2)}) collective-permute-start(bf16[256,64]{0,1:T(8,128)(2,1)S(1)} %bitcast.240), channel_id=1, source_target_pairs={{2,0},{3,1},{4,2},{5,3},{6,4},{7,5},{8,6},{9,7},{10,8},{11,9},{12,... | collective-permute-start | bytes 98312 | tf_op jit(solution)/shard_map/ppermute | solution.py:14
  253.3 0.9 collective-permute-done.7
  254.3 0.7 copy-done.4
  255.0 2.2 convolution_convert_fusion.2
  257.3 1.9 collective-permute-start.8
  259.2 1.0 fusion.72
  260.1 1.9 collective-permute-start.10
  262.1 3.6 %collective-permute-start.9 = (bf16[256,64]{0,1:T(8,128)(2,1)}, bf16[256,64]{0,1:T(8,128)(2,1)S(1)}, u32[]{:S(2)}, u32[]{:S(2)}) collective-permute-start(bf16[256,64]{0,1:T(8,128)(2,1)} %bitcast.44), channel_id=1, source_target_pairs={{0,1},{1,2},{2,3},{3,4},{4,5},{5,6},{6,7},{7,8},{8,9},{9,10},{10,1... | collective-permute-start | bytes 98312 | tf_op jit(solution)/shard_map/ppermute | solution.py:14
  265.7 12.1 %collective-permute-start.11 = (bf16[256,64]{0,1:T(8,128)(2,1)}, bf16[256,64]{0,1:T(8,128)(2,1)S(1)}, u32[]{:S(2)}, u32[]{:S(2)}) collective-permute-start(bf16[256,64]{0,1:T(8,128)(2,1)} %bitcast.44), channel_id=1, source_target_pairs={{2,0},{3,1},{4,2},{5,3},{6,4},{7,5},{8,6},{9,7},{10,8},{11,9},{12,... | collective-permute-start | bytes 98312 | tf_op jit(solution)/shard_map/ppermute | solution.py:14
  277.8 0.8 constant_dynamic-update-slice_fusion.7
  278.6 0.5 collective-permute-done.11
  279.2 2.2 convolution_convert_fusion.1
  281.4 1.9 collective-permute-start.12
  283.4 1.0 fusion.71
  284.3 1.9 collective-permute-start.14
  286.2 3.6 %collective-permute-start.13 = (bf16[256,64]{0,1:T(8,128)(2,1)}, bf16[256,64]{0,1:T(8,128)(2,1)S(1)}, u32[]{:S(2)}, u32[]{:S(2)}) collective-permute-start(bf16[256,64]{0,1:T(8,128)(2,1)} %bitcast.58), channel_id=1, source_target_pairs={{0,1},{1,2},{2,3},{3,4},{4,5},{5,6},{6,7},{7,8},{8,9},{9,10},{10,1... | collective-permute-start | bytes 98312 | tf_op jit(solution)/shard_map/ppermute | solution.py:14
  289.9 12.0 %collective-permute-start.15 = (bf16[256,64]{0,1:T(8,128)(2,1)}, bf16[256,64]{0,1:T(8,128)(2,1)S(1)}, u32[]{:S(2)}, u32[]{:S(2)}) collective-permute-start(bf16[256,64]{0,1:T(8,128)(2,1)} %bitcast.58), channel_id=1, source_target_pairs={{2,0},{3,1},{4,2},{5,3},{6,4},{7,5},{8,6},{9,7},{10,8},{11,9},{12,... | collective-permute-start | bytes 98312 | tf_op jit(solution)/shard_map/ppermute | solution.py:14
  301.9 0.8 constant_dynamic-update-slice_fusion.12
  302.7 0.5 collective-permute-done.15
  303.3 1.6 fusion.54
  304.9 1.4 maximum_bitcast_fusion
  (59 shorter events, 0.6 us)
Async XLA Ops:
  6.5 225.7 %copy-start = (bf16[1,3,5,256,256]{4,3,2,1,0:T(8,128)(2,1)S(1)}, bf16[1,3,5,256,256]{4,3,2,1,0:T(8,128)(2,1)}, u32[]{:S(2)}) copy-start(bf16[1,3,5,256,256]{4,3,2,1,0:T(8,128)(2,1)} %param.16) | copy-start | bytes 5898244
  9.2 54.7 %all-to-all-start = ((bf16[8,1,8,256,64]{3,4,2,1,0:T(8,128)(2,1)}), bf16[8,1,8,256,64]{3,4,2,1,0:T(8,128)(2,1)}, u32[]{:S(2)}, u32[]{:S(2)}) async-start(bf16[8,1,8,256,64]{3,4,2,1,0:T(8,128)(2,1)} %broadcast_in_dim.31), calls=%async_computation | async-start | bytes 4194304 | tf_op jit(solution)/shard_map/all_to_all | solution.py:19
  15.7 161.2 %reduce-scatter.4.cloned.1.call-start = ((), (), s32[]{:S(2)}) async-start(), calls=%async_computation.4 | async-start | bytes 5242880 | tf_op jit(solution)/shard_map/reduce_scatter | solution.py:41
  63.9 11.7 %copy-start.6 = (f32[1,64]{1,0:T(1,128)S(1)}, f32[1,64]{1,0:T(1,128)}, u32[]{:S(2)}) copy-start(f32[1,64]{1,0:T(1,128)} %param.15) | copy-start | bytes 772
  91.6 8.2 %copy-start.1 = (bf16[4,64,256,64]{2,3,0,1:T(8,128)(2,1)S(1)}, bf16[4,64,256,64]{2,3,0,1:T(8,128)(2,1)}, u32[]{:S(2)}) copy-start(bf16[4,64,256,64]{2,3,0,1:T(8,128)(2,1)} %get-tuple-element.5) | copy-start | bytes 25165828
  91.6 8.2 %copy-start.7 = (s32[1,64]{1,0:T(1,128)S(1)}, s32[1,64]{1,0:T(1,128)}, u32[]{:S(2)}) copy-start(s32[1,64]{1,0:T(1,128)} %param.12) | copy-start | bytes 772
  120.5 56.5 %copy-start.3 = (bf16[1,8,256,64]{2,3,1,0:T(8,128)(2,1)S(1)}, bf16[1,8,256,64]{2,3,1,0:T(8,128)(2,1)}, u32[]{:S(2)}) copy-start(bf16[1,8,256,64]{2,3,1,0:T(8,128)(2,1)} %param.10) | copy-start | bytes 786436
  120.5 111.8 %copy-start.2 = (bf16[1,256,256]{2,1,0:T(8,128)(2,1)S(1)}, bf16[1,256,256]{2,1,0:T(8,128)(2,1)}, u32[]{:S(2)}) copy-start(bf16[1,256,256]{2,1,0:T(8,128)(2,1)} %param.17) | copy-start | bytes 393220
  127.2 78.3 %reduce-scatter.6.cloned.1.call-start = ((), (), s32[]{:S(2)}) async-start(), calls=%async_computation.5 | async-start | bytes 1310720 | tf_op jit(solution)/shard_map/reduce_scatter | solution.py:41
  177.0 54.4 %reduce-scatter.8.cloned.1.call-start = ((), (), s32[]{:S(2)}) async-start(), calls=%async_computation.6 | async-start | bytes 393216 | tf_op jit(solution)/shard_map/reduce_scatter | solution.py:41
  177.1 15.9 %collective-permute-start = (bf16[3,256,64]{1,2,0:T(8,128)(2,1)S(1)}, bf16[3,256,64]{1,2,0:T(8,128)(2,1)S(1)}, u32[]{:S(2)}, u32[]{:S(2)}) collective-permute-start(bf16[3,256,64]{1,2,0:T(8,128)(2,1)S(1)} %slice_bitcast_fusion), channel_id=1, source_target_pairs={{0,2},{1,3},{2,4},{3,5},{4,6},{5,7},{6,8},{7,9},{8,10},{9,11},{10,... | collective-permute-start | bytes 294920 | tf_op jit(solution)/shard_map/ppermute | solution.py:14
  180.2 25.3 %collective-permute-start.3 = (bf16[3,256,64]{1,2,0:T(8,128)(2,1)S(1)}, bf16[3,256,64]{1,2,0:T(8,128)(2,1)S(1)}, u32[]{:S(2)}, u32[]{:S(2)}) collective-permute-start(bf16[3,256,64]{1,2,0:T(8,128)(2,1)S(1)} %slice_bitcast_fusion), channel_id=1, source_target_pairs={{2,0},{3,1},{4,2},{5,3},{6,4},{7,5},{8,6},{9,7},{10,8},{11,9},{12,... | collective-permute-start | bytes 294920 | tf_op jit(solution)/shard_map/ppermute | solution.py:14
  187.3 18.2 %collective-permute-start.2 = (bf16[3,256,64]{1,2,0:T(8,128)(2,1)S(1)}, bf16[3,256,64]{1,2,0:T(8,128)(2,1)S(1)}, u32[]{:S(2)}, u32[]{:S(2)}) collective-permute-start(bf16[3,256,64]{1,2,0:T(8,128)(2,1)S(1)} %slice_bitcast_fusion), channel_id=1, source_target_pairs={{1,0},{2,1},{3,2},{4,3},{5,4},{6,5},{7,6},{8,7},{9,8},{10,9},{11,1... | collective-permute-start | bytes 294920 | tf_op jit(solution)/shard_map/ppermute | solution.py:14
  190.3 4.2 %collective-permute-start.1 = (bf16[3,256,64]{1,2,0:T(8,128)(2,1)S(1)}, bf16[3,256,64]{1,2,0:T(8,128)(2,1)S(1)}, u32[]{:S(2)}, u32[]{:S(2)}) collective-permute-start(bf16[3,256,64]{1,2,0:T(8,128)(2,1)S(1)} %slice_bitcast_fusion), channel_id=1, source_target_pairs={{0,1},{1,2},{2,3},{3,4},{4,5},{5,6},{6,7},{7,8},{8,9},{9,10},{10,1... | collective-permute-start | bytes 294920 | tf_op jit(solution)/shard_map/ppermute | solution.py:14
  233.9 19.3 %collective-permute-start.4 = (bf16[256,64]{0,1:T(8,128)(2,1)S(1)}, bf16[256,64]{0,1:T(8,128)(2,1)S(1)}, u32[]{:S(2)}, u32[]{:S(2)}) collective-permute-start(bf16[256,64]{0,1:T(8,128)(2,1)S(1)} %bitcast.237), channel_id=1, source_target_pairs={{0,2},{1,3},{2,4},{3,5},{4,6},{5,7},{6,8},{7,9},{8,10},{9,11},{10,... | collective-permute-start | bytes 98312 | tf_op jit(solution)/shard_map/ppermute | solution.py:14
  239.1 14.3 %collective-permute-start.6 = (bf16[256,64]{0,1:T(8,128)(2,1)S(1)}, bf16[256,64]{0,1:T(8,128)(2,1)S(1)}, u32[]{:S(2)}, u32[]{:S(2)}) collective-permute-start(bf16[256,64]{0,1:T(8,128)(2,1)S(1)} %bitcast.238), channel_id=1, source_target_pairs={{1,0},{2,1},{3,2},{4,3},{5,4},{6,5},{7,6},{8,7},{9,8},{10,9},{11,1... | collective-permute-start | bytes 98312 | tf_op jit(solution)/shard_map/ppermute | solution.py:14
  242.0 11.3 %collective-permute-start.5 = (bf16[256,64]{0,1:T(8,128)(2,1)S(1)}, bf16[256,64]{0,1:T(8,128)(2,1)S(1)}, u32[]{:S(2)}, u32[]{:S(2)}) collective-permute-start(bf16[256,64]{0,1:T(8,128)(2,1)S(1)} %bitcast.239), channel_id=1, source_target_pairs={{0,1},{1,2},{2,3},{3,4},{4,5},{5,6},{6,7},{7,8},{8,9},{9,10},{10,1... | collective-permute-start | bytes 98312 | tf_op jit(solution)/shard_map/ppermute | solution.py:14
  244.6 9.6 %collective-permute-start.7 = (bf16[256,64]{0,1:T(8,128)(2,1)S(1)}, bf16[256,64]{0,1:T(8,128)(2,1)S(1)}, u32[]{:S(2)}, u32[]{:S(2)}) collective-permute-start(bf16[256,64]{0,1:T(8,128)(2,1)S(1)} %bitcast.240), channel_id=1, source_target_pairs={{2,0},{3,1},{4,2},{5,3},{6,4},{7,5},{8,6},{9,7},{10,8},{11,9},{12,... | collective-permute-start | bytes 98312 | tf_op jit(solution)/shard_map/ppermute | solution.py:14
  254.3 0.7 copy-start.4
  257.3 20.5 %collective-permute-start.8 = (bf16[256,64]{0,1:T(8,128)(2,1)}, bf16[256,64]{0,1:T(8,128)(2,1)S(1)}, u32[]{:S(2)}, u32[]{:S(2)}) collective-permute-start(bf16[256,64]{0,1:T(8,128)(2,1)} %bitcast.44), channel_id=1, source_target_pairs={{0,2},{1,3},{2,4},{3,5},{4,6},{5,7},{6,8},{7,9},{8,10},{9,11},{10,... | collective-permute-start | bytes 98312 | tf_op jit(solution)/shard_map/ppermute | solution.py:14
  260.1 18.5 %collective-permute-start.10 = (bf16[256,64]{0,1:T(8,128)(2,1)}, bf16[256,64]{0,1:T(8,128)(2,1)S(1)}, u32[]{:S(2)}, u32[]{:S(2)}) collective-permute-start(bf16[256,64]{0,1:T(8,128)(2,1)} %bitcast.44), channel_id=1, source_target_pairs={{1,0},{2,1},{3,2},{4,3},{5,4},{6,5},{7,6},{8,7},{9,8},{10,9},{11,1... | collective-permute-start | bytes 98312 | tf_op jit(solution)/shard_map/ppermute | solution.py:14
  262.1 15.8 %collective-permute-start.9 = (bf16[256,64]{0,1:T(8,128)(2,1)}, bf16[256,64]{0,1:T(8,128)(2,1)S(1)}, u32[]{:S(2)}, u32[]{:S(2)}) collective-permute-start(bf16[256,64]{0,1:T(8,128)(2,1)} %bitcast.44), channel_id=1, source_target_pairs={{0,1},{1,2},{2,3},{3,4},{4,5},{5,6},{6,7},{7,8},{8,9},{9,10},{10,1... | collective-permute-start | bytes 98312 | tf_op jit(solution)/shard_map/ppermute | solution.py:14
  265.7 13.4 %collective-permute-start.11 = (bf16[256,64]{0,1:T(8,128)(2,1)}, bf16[256,64]{0,1:T(8,128)(2,1)S(1)}, u32[]{:S(2)}, u32[]{:S(2)}) collective-permute-start(bf16[256,64]{0,1:T(8,128)(2,1)} %bitcast.44), channel_id=1, source_target_pairs={{2,0},{3,1},{4,2},{5,3},{6,4},{7,5},{8,6},{9,7},{10,8},{11,9},{12,... | collective-permute-start | bytes 98312 | tf_op jit(solution)/shard_map/ppermute | solution.py:14
  279.1 2.3 copy-start.5
  281.4 20.4 %collective-permute-start.12 = (bf16[256,64]{0,1:T(8,128)(2,1)}, bf16[256,64]{0,1:T(8,128)(2,1)S(1)}, u32[]{:S(2)}, u32[]{:S(2)}) collective-permute-start(bf16[256,64]{0,1:T(8,128)(2,1)} %bitcast.58), channel_id=1, source_target_pairs={{0,2},{1,3},{2,4},{3,5},{4,6},{5,7},{6,8},{7,9},{8,10},{9,11},{10,... | collective-permute-start | bytes 98312 | tf_op jit(solution)/shard_map/ppermute | solution.py:14
  284.3 18.4 %collective-permute-start.14 = (bf16[256,64]{0,1:T(8,128)(2,1)}, bf16[256,64]{0,1:T(8,128)(2,1)S(1)}, u32[]{:S(2)}, u32[]{:S(2)}) collective-permute-start(bf16[256,64]{0,1:T(8,128)(2,1)} %bitcast.58), channel_id=1, source_target_pairs={{1,0},{2,1},{3,2},{4,3},{5,4},{6,5},{7,6},{8,7},{9,8},{10,9},{11,1... | collective-permute-start | bytes 98312 | tf_op jit(solution)/shard_map/ppermute | solution.py:14
  286.2 15.7 %collective-permute-start.13 = (bf16[256,64]{0,1:T(8,128)(2,1)}, bf16[256,64]{0,1:T(8,128)(2,1)S(1)}, u32[]{:S(2)}, u32[]{:S(2)}) collective-permute-start(bf16[256,64]{0,1:T(8,128)(2,1)} %bitcast.58), channel_id=1, source_target_pairs={{0,1},{1,2},{2,3},{3,4},{4,5},{5,6},{6,7},{7,8},{8,9},{9,10},{10,1... | collective-permute-start | bytes 98312 | tf_op jit(solution)/shard_map/ppermute | solution.py:14
  289.9 13.3 %collective-permute-start.15 = (bf16[256,64]{0,1:T(8,128)(2,1)}, bf16[256,64]{0,1:T(8,128)(2,1)S(1)}, u32[]{:S(2)}, u32[]{:S(2)}) collective-permute-start(bf16[256,64]{0,1:T(8,128)(2,1)} %bitcast.58), channel_id=1, source_target_pairs={{2,0},{3,1},{4,2},{5,3},{6,4},{7,5},{8,6},{9,7},{10,8},{11,9},{12,... | collective-permute-start | bytes 98312 | tf_op jit(solution)/shard_map/ppermute | solution.py:14
Sparse Core Ops, SparseCore 0:
  127.3 49.6 reduce-scatter.3
  179.5 25.9 reduce-scatter.5
  208.0 23.3 reduce-scatter.7
where the time goes:
time: 314 us; the launch traced here: 313 us
  waiting for transfers between devices  137 us (44%)
  starting transfers between devices  80.8 us (26%)
  matrix products  37.4 us (12%)
  local copies, waits for them, and re-layouts  30.8 us (10%)
  other arithmetic  13.6 us (4%)
  between operations  13.5 us (4%)
    reduce_scatter x3, waiting for transfers between devices, sum_in_order(): blocks = lax.psum_scatter(blocks, axes[k], scatter_dimension=0, tiled=True)  86.4 us
    ppermute x16, starting transfers between devices, shifted(): return lax.ppermute(block, axis, route)  74.1 us
    all_to_all x1, waiting for transfers between devices, sent_to_all(): lax.all_to_all(jnp.broadcast_to(value[None], (size, *value.shape)), axis,...  46.8 us
    dot_general x1, matrix products, on_device(): jnp.einsum('kij,skjr->skir', hist_tiles[0], picked, preferred_element_typ...  15.9 us
    gather x1, local copies, waits for them, and re-layouts, on_device(): picked = group_past[tile_cols[0][None, :], when]  11.7 us
    convert_element_type x1, other arithmetic, on_device(): terms_high = terms.astype(jnp.bfloat16)  7.87 us
    dot_general x1, matrix products, on_device(): jnp.einsum('gk,skir->gsir', onehot, terms_high, preferred_element_type=jn...  7.8 us
    dot_general x4, matrix products, on_device(): jnp.dot(inverses[0], rhs, preferred_element_type=jnp.float32)  7.69 us
  transfers between devices with their start and end apart: 20, of which 8 were waited for; matrix products, arithmetic and copies ran while one was open for 2% of the time, Pallas kernels for 0%

commit v1 on v0

v1 whole, which is shorter than its diff:
```python
import functools

import jax
import jax.numpy as jnp
from jax import lax
from jax.experimental import pallas as pl
from jax.experimental.pallas import tpu as pltpu
from jax.sharding import Mesh
from jax.sharding import PartitionSpec as P

AXES = ("hist_0", "hist_1", "hist_2", "row", "cur")
MESH = pl.DeviceIdType.MESH
F32 = jnp.float32
BF16 = jnp.bfloat16
STEPS = 4
HALF = 32
ILLUM = 64
BLOCK = 256
TILES = 64
GROUPS = 32
PATCHES = 256
TILE_PARTS = 8


def times_transposed(x, w):
    return lax.dot_general(x, w, (((1,), (1,)), ((), ())), preferred_element_type=F32)


def kernel(
    info_ref, scale_ref, end_ref,
    past_ref, tiles_ref, near_ref, inverse_ref, incident_ref,
    out_ref,
    tiles, near, inverse, incident, gp, acc, slots, pa, pb,
    rel1, dir1, s1, rel2, dir2, ts, hist, zr, window, fresh, pre,
    local_sem, g_send, g_recv, d_send, d_recv,
    r_send, r_recv, z_send, z_recv, w_send, w_recv, n_send, n_recv,
):
    x = lax.axis_index("hist_0")
    zh = lax.axis_index("hist_1")
    y = lax.axis_index("hist_2")
    row = lax.axis_index("row")
    cur = lax.axis_index("cur")
    me = (((x * 2 + zh) * 4 + y) * 4 + row) * 2 + cur
    own = row * 2 + cur

    def patch_device(offset):
        q = lax.rem(me + offset + PATCHES, PATCHES)
        return {
            "hist_0": q // 64,
            "hist_1": lax.rem(q // 32, 2),
            "hist_2": lax.rem(q // 8, 4),
            "row": lax.rem(q // 2, 4),
            "cur": lax.rem(q, 2),
        }

    barrier = pltpu.get_barrier_semaphore()

    first = pltpu.make_async_copy(past_ref, gp.at[own], local_sem.at[0])
    first.start()
    loads = []
    part = TILES // TILE_PARTS
    for k in range(TILE_PARTS):
        loads.append(
            pltpu.make_async_copy(
                tiles_ref.at[pl.ds(k * part, part)],
                tiles.at[pl.ds(k * part, part)],
                local_sem.at[4 + k],
            )
        )
    near_load = pltpu.make_async_copy(near_ref, near, local_sem.at[1])
    inverse_load = pltpu.make_async_copy(inverse_ref, inverse, local_sem.at[2])
    incident_load = pltpu.make_async_copy(incident_ref, incident, local_sem.at[3])

    partners = [
        {"hist_0": lax.rem(x + 1, 4)},
        {"hist_0": lax.rem(x + 3, 4)},
        {"hist_2": lax.rem(y + 1, 4)},
        {"hist_2": lax.rem(y + 3, 4)},
        {"hist_1": 1 - zh},
        {"row": lax.rem(row + 1, 4)},
        {"row": lax.rem(row + 2, 4)},
        {"row": lax.rem(row + 3, 4)},
        {"cur": 1 - cur},
        patch_device(1),
        patch_device(2),
        patch_device(-1),
        patch_device(-2),
    ]
    for device in partners:
        pl.semaphore_signal(barrier, inc=1, device_id=device, device_id_type=MESH)
    pl.semaphore_wait(barrier, len(partners))
    first.wait()

    def remote(src, dst, send, recv, device):
        return pltpu.make_async_remote_copy(
            src_ref=src, dst_ref=dst, send_sem=send, recv_sem=recv,
            device_id=device, device_id_type=MESH,
        )

    inner = lax.rem((row + 1) // 2, 2)
    opposite = lax.rem(row + 2, 4)
    middle = 1 + lax.rem(row, 2)
    outer = 3 * (row // 2)
    blocks = [opposite, 1 + lax.rem(row, 2), 3 - 3 * lax.rem(row, 2)]
    to_opposite = remote(gp.at[own], gp.at[own], g_send.at[0], g_recv.at[0], {"row": opposite})
    to_middle = remote(
        gp.at[own], gp.at[own], g_send.at[1], g_recv.at[2 - inner], {"row": middle}
    )
    to_outer = remote(gp.at[own], gp.at[own], g_send.at[2], g_recv.at[1], {"row": outer})
    far = opposite * 2 + cur
    relayed = remote(gp.at[far], gp.at[far], g_send.at[3], g_recv.at[2], {"row": outer})
    to_opposite.start()
    to_middle.start()

    @pl.when(inner == 1)
    def _():
        to_outer.start()

    across = []
    for k, block in enumerate([row] + blocks):
        spot = gp.at[block * 2 + cur]
        across.append(remote(spot, spot, d_send.at[k], d_recv.at[k], {"cur": 1 - cur}))
    across[0].start()
    for load in loads:
        load.start()
    near_load.start()
    inverse_load.start()
    incident_load.start()

    def arrived(k):
        spot = gp.at[blocks[k] * 2 + cur]
        remote(spot, spot, g_send.at[k], g_recv.at[k], {"row": opposite}).wait_recv()

    arrived(0)

    @pl.when(inner == 1)
    def _():
        relayed.start()

    across[1].start()

    offsets = (-2, -1, 1, 2)
    window_sends = []
    for k, o in enumerate(offsets):
        window_sends.append(
            remote(
                gp.at[own, pl.ds(5, 3)], window.at[o + 2, pl.ds(0, 3)],
                w_send.at[k], w_recv.at[k], patch_device(-o),
            )
        )
    arrived(1)
    across[2].start()
    arrived(2)
    across[3].start()
    for send in window_sends:
        send.start()
    window[2, pl.ds(0, 3)] = gp[own, pl.ds(5, 3)]
    for load in loads:
        load.wait()
    for copy in across:
        copy.wait_recv()

    acc[...] = jnp.zeros_like(acc)

    def one_tile(k, carry):
        tile = info_ref[0, k]
        col = info_ref[1, k]
        begin = info_ref[2, k]
        held = gp[col, pl.ds(begin, STEPS)].reshape(STEPS * ILLUM, BLOCK)
        term = times_transposed(held, tiles[tile]) * scale_ref[0, k]
        total = acc[...] * scale_ref[1, k] + term
        acc[...] = total
        slots[k] = total.astype(BF16)
        return carry

    lax.fori_loop(0, TILES, one_tile, 0, unroll=2)

    def spread(t):
        def one_group(g, carry):
            end = end_ref[0, g]
            there = end_ref[1, g]
            value = slots[end, pl.ds(t * ILLUM, ILLUM)]
            value = jnp.where(there > 0, value, jnp.zeros_like(value))
            gx = g // 8
            gz = lax.rem(g // 4, 2)
            gy = lax.rem(g, 4)
            pa[t, gx, gz, gy] = value[:HALF]
            pb[t, gy, gz, gx] = value[HALF:]
            return carry

        lax.fori_loop(0, GROUPS, one_group, 0, unroll=4)

    rings = (("hist_0", x), ("hist_2", y))
    sends = []

    def ring_copy(t, stage, h, n, src, dst, device):
        index = ((t * 2 + stage) * 2 + h) * 6 + n
        copy = remote(src, dst, r_send.at[index], r_recv.at[index], device)
        sends.append(copy)
        return copy

    def ring(t, stage, h):
        axis, i = rings[(h + stage) % 2]
        right, left, over = lax.rem(i + 1, 4), lax.rem(i + 3, 4), lax.rem(i + 2, 4)
        if stage == 0:
            source = (pa, pb)[h]
            at = lambda j, z: source.at[t, j, z]
            rel, dirs = rel1, dir1
        else:
            at = lambda j, z: s1.at[h, t, z, j]
            rel, dirs = rel2, dir2
        to_right, to_left = {axis: right}, {axis: left}
        copies = (
            ring_copy(t, stage, h, 0, at(over, 0), rel.at[h, 0, t], to_right),
            ring_copy(t, stage, h, 1, at(over, 1), rel.at[h, 1, t], to_left),
            ring_copy(t, stage, h, 2, at(right, 1), dirs.at[h, 0, t, 1], to_right),
            ring_copy(t, stage, h, 3, at(left, 0), dirs.at[h, 1, t, 0], to_left),
            ring_copy(t, stage, h, 4, at(right, 0), dirs.at[h, 0, t, 0], to_right),
            ring_copy(t, stage, h, 5, at(left, 1), dirs.at[h, 1, t, 1], to_left),
        )
        return copies, at, rel, dirs, right, left, i

    state = {}

    def start(t, stage):
        for h in (0, 1):
            state[t, stage, h] = ring(t, stage, h)
        for n in (0, 1, 2, 3):
            for h in (0, 1):
                state[t, stage, h][0][n].start()

    def relay(t, stage):
        for n, z in ((0, 0), (1, 1)):
            for h in (0, 1):
                copies, at, rel, dirs, right, left, i = state[t, stage, h]
                copies[n].wait_recv()
                spot = at((right, left)[n], z)
                spot[...] = (spot[...].astype(F32) + rel[h, n, t].astype(F32)).astype(BF16)
                copies[4 + n].start()

    def finish_first(t):
        for h in (0, 1):
            copies, at, rel, dirs, right, left, i = state[t, 0, h]
            for n in (2, 3, 4, 5):
                copies[n].wait_recv()
            for z in (0, 1):
                total = at(i, z)[...].astype(F32) + dirs[h, 0, t, z].astype(F32)
                s1[h, t, z] = (total + dirs[h, 1, t, z].astype(F32)).astype(BF16)

    pairs = {}

    def finish_second(t):
        for h in (0, 1):
            copies, at, rel, dirs, right, left, i = state[t, 1, h]
            for n in (2, 3, 4, 5):
                copies[n].wait_recv()

        def total(h, z):
            copies, at, rel, dirs, right, left, i = state[t, 1, h]
            return at(i, z)[...].astype(F32) + dirs[h, 0, t, z].astype(F32) + dirs[h, 1, t, z].astype(F32)

        for h in (0, 1):
            ts[t, pl.ds(h * HALF, HALF)] = total(h, 1 - zh).astype(BF16)
        pairs[t] = remote(ts.at[t], zr.at[t], z_send.at[t], z_recv.at[t], {"hist_1": 1 - zh})
        sends.append(pairs[t])
        pairs[t].start()
        for h in (0, 1):
            hist[t, pl.ds(h * HALF, HALF)] = total(h, zh)

    valid = {o: jnp.logical_and(me + o >= 0, me + o < PATCHES) for o in offsets}

    def beside(o, s):
        value = window[o + 2, s + 3]
        if o == 0:
            return value
        return jnp.where(valid[o], value, jnp.zeros_like(value))

    def near_sum(lag, s, chosen):
        total = None
        for o in chosen:
            term = times_transposed(beside(o, s), near[(lag - 1) * 5 + o + 2])
            total = term if total is None else total + term
        return total

    everyone = (-2, -1, 0, 1, 2)
    rounds = {}

    def start_pre():
        near_load.wait()
        inverse_load.wait()
        incident_load.wait()
        for send in window_sends:
            send.wait_recv()
        for t in range(STEPS):
            total = incident[t].astype(F32)
            for lag in range(1, 4):
                if t - lag < 0:
                    total = total - near_sum(lag, t - lag, everyone)
            pre[t] = total

    def near_step(t):
        total = pre[t]
        if t > 0:
            for copy in rounds[t - 1]:
                copy.wait_recv()
            total = total - near_sum(1, t - 1, offsets)
        if t == 0 or True:
            pairs[t].wait_recv()
        rhs = (total - hist[t] - zr[t].astype(F32)).astype(BF16)
        made = times_transposed(rhs, inverse[...]).astype(BF16)
        out_ref[t] = made
        if t + 1 < STEPS:
            fresh[t] = made
            rounds[t] = []
            for k, o in enumerate(offsets):
                copy = remote(
                    fresh.at[t], window.at[o + 2, t + 3],
                    n_send.at[t * 4 + k], n_recv.at[t * 4 + k], patch_device(-o),
                )
                copy.start()
                rounds[t].append(copy)
                sends.append(copy)
            window[2, t + 3] = made
            pre[t + 1] = pre[t + 1] - near_sum(1, t, (0,))
        if t > 0:
            for lag in (2, 3):
                if t - 1 + lag < STEPS:
                    pre[t - 1 + lag] = pre[t - 1 + lag] - near_sum(lag, t - 1, everyone)

    spread(0)
    start(0, 0)
    spread(1)
    start(1, 0)
    spread(2)
    spread(3)
    relay(0, 0)
    start(2, 0)
    relay(1, 0)
    finish_first(0)
    start(0, 1)
    start(3, 0)
    start_pre()
    relay(2, 0)
    relay(0, 1)
    finish_first(1)
    start(1, 1)
    finish_second(0)
    relay(3, 0)
    relay(1, 1)
    finish_first(2)
    start(2, 1)
    near_step(0)
    finish_second(1)
    relay(2, 1)
    finish_first(3)
    start(3, 1)
    near_step(1)
    finish_second(2)
    relay(3, 1)
    near_step(2)
    finish_second(3)
    near_step(3)

    for copy in sends:
        copy.wait_send()
    for copy in window_sends:
        copy.wait_send()
    for copy in across:
        copy.wait_send()
    to_opposite.wait_send()
    to_middle.wait_send()

    @pl.when(inner == 1)
    def _():
        to_outer.wait_send()
        relayed.wait_send()


def in_target_order(tile_rows, tile_cols, tile_lags, tile_scales, kept):
    ids = jnp.arange(TILES, dtype=jnp.int32)
    key = tile_rows * TILES + ids
    rank = jnp.sum((key[None, :] < key[:, None]).astype(jnp.int32), axis=1)
    at = rank[None, :] == ids[:, None]

    def placed(value):
        return jnp.sum(jnp.where(at, value[None, :], jnp.zeros_like(value)[None, :]), axis=1)

    same = (tile_rows[None, :] == tile_rows[:, None]) & (ids[None, :] < ids[:, None])
    goes_on = jnp.any(same, axis=1).astype(F32)
    info = jnp.stack([placed(ids), placed(tile_cols), placed(kept - tile_lags)])
    scales = jnp.stack([placed(tile_scales), placed(goes_on)])
    groups = jnp.arange(GROUPS, dtype=jnp.int32)
    upto = jnp.sum((tile_rows[None, :] <= groups[:, None]).astype(jnp.int32), axis=1)
    count = jnp.sum((tile_rows[None, :] == groups[:, None]).astype(jnp.int32), axis=1)
    ends = jnp.stack([jnp.maximum(upto - 1, 0), count])
    return info, scales, ends


def on_device(
    incident, past, hist_tiles, tile_rows, tile_cols, tile_lags, tile_scales, near_tiles, inverses
):
    kept = past.shape[1]
    info, scales, ends = in_target_order(
        tile_rows[0], tile_cols[0], tile_lags[0], tile_scales[0], kept
    )
    dma = pltpu.SemaphoreType.DMA
    vmem = pltpu.VMEM
    smem_spec = pl.BlockSpec(memory_space=pltpu.SMEM)
    any_spec = pl.BlockSpec(memory_space=pl.ANY)
    made = pl.pallas_call(
        kernel,
        out_shape=jax.ShapeDtypeStruct((STEPS, ILLUM, BLOCK), BF16),
        in_specs=[smem_spec] * 3 + [any_spec] * 5,
        out_specs=pl.BlockSpec(memory_space=pltpu.VMEM),
        scratch_shapes=[
            vmem((TILES, BLOCK, BLOCK), BF16),
            vmem((15, BLOCK, BLOCK), BF16),
            vmem((BLOCK, BLOCK), BF16),
            vmem((STEPS, ILLUM, BLOCK), BF16),
            vmem((8, kept, ILLUM, BLOCK), BF16),
            vmem((STEPS * ILLUM, BLOCK), F32),
            vmem((TILES, STEPS * ILLUM, BLOCK), BF16),
            vmem((STEPS, 4, 2, 4, HALF, BLOCK), BF16),
            vmem((STEPS, 4, 2, 4, HALF, BLOCK), BF16),
            vmem((2, 2, STEPS, 4, HALF, BLOCK), BF16),
            vmem((2, 2, STEPS, 2, 4, HALF, BLOCK), BF16),
            vmem((2, STEPS, 2, 4, HALF, BLOCK), BF16),
            vmem((2, 2, STEPS, HALF, BLOCK), BF16),
            vmem((2, 2, STEPS, 2, HALF, BLOCK), BF16),
            vmem((STEPS, ILLUM, BLOCK), BF16),
            vmem((STEPS, ILLUM, BLOCK), F32),
            vmem((STEPS, ILLUM, BLOCK), BF16),
            vmem((5, 6, ILLUM, BLOCK), BF16),
            vmem((3, ILLUM, BLOCK), BF16),
            vmem((STEPS, ILLUM, BLOCK), F32),
            dma((4 + TILE_PARTS,)),
            dma((4,)), dma((3,)), dma((4,)), dma((4,)),
            dma((96,)), dma((96,)), dma((4,)), dma((4,)),
            dma((4,)), dma((4,)), dma((12,)), dma((12,)),
        ],
        compiler_params=pltpu.CompilerParams(
            collective_id=0, has_side_effects=True, vmem_limit_bytes=58 * 1024 * 1024
        ),
    )(
        info, scales, ends,
        jnp.swapaxes(past[0], 1, 2),
        hist_tiles[0],
        near_tiles[0].reshape(15, BLOCK, BLOCK),
        inverses[0],
        jnp.swapaxes(incident[:, 0], 1, 2),
    )
    return jnp.swapaxes(made, 1, 2)[:, None]


def solution(mesh):
    torus = Mesh(
        mesh.devices.reshape(4, 2, 4, mesh.shape["row"], mesh.shape["cur"]), AXES
    )
    placed = (
        P(None, AXES, None, None),
        P(AXES, None, None, None),
        P(AXES, None, None, None),
        P(AXES, None),
        P(AXES, None),
        P(AXES, None),
        P(AXES, None),
        P(AXES, None, None, None, None),
        P(AXES, None, None),
    )
    return jax.shard_map(
        on_device,
        mesh=torus,
        in_specs=placed,
        out_specs=P(None, AXES, None, None),
        check_vma=False,
    )
```

time: 314 us -> 95.9 us (0.31)
  the two profiles are of different devices: /device:TPU:3 before, /device:TPU:24 now
where the time goes in v1:
time: 95.9 us; the launch traced here: 95.8 us
  Pallas kernels  87 us (91%)
  other arithmetic  7.2 us (8%)
  local copies, waits for them, and re-layouts  1.57 us (2%)
    pallas_call x1, Pallas kernels, on_device(): pl.pallas_call(kernel, out_shape=jax.ShapeDtypeStruct((STEPS, ILLUM, BLOC...  87 us

profile of v1, /device:TPU:24, one launch (start us, length us, event | category | flops | bytes accessed | tf_op | source)
XLA Modules:
  0.0 95.8 jit_solution(3771343438755572123)
XLA Ops:
  0.0 0.7 subtract_bitcast_fusion
  0.7 0.9 fusion.1
  1.6 0.7 iota_add_fusion
  2.2 0.7 add_bitcast_fusion
  2.9 0.2 convert_reduce_fusion
  3.1 0.8 select_reduce_fusion.1
  3.9 0.6 pad_maximum_fusion.scale_ref
  4.5 0.8 select_reduce_fusion.4
  5.3 0.6 pad_add_fusion.info_ref
  5.9 0.8 convert_reduce_fusion.2
  6.6 0.6 pad_add_fusion.1.end_ref
  7.2 87.0 %shard_map.91 = bf16[4,64,256]{2,1,0:T(8,128)(2,1)} custom-call(s32[3,64]{1,0:T(4,128)} %pad_add_fusion.info_ref, f32[2,64]{1,0:T(2,128)} %pad_maximum_fusion.scale_ref, s32[2,32]{1,0:T(2,128)} %pad_add_fusion.1.end_ref, bf16[8,64,256]{2,1,0:T(8,128)(2,1)} %bitcast.33, bf16[64,256,256]{2,1,0:T(8,128)(2,1)} %bitcast.30, bf16[15,256,256]{2,1,0:T(8,128)(2,1)} %bitcast.31, ...), custom_call_target="tpu_custom_call" | custom-call | tf_op jit(solution)/shard_map/pallas_call | solution.py:410
  94.2 1.6 %copy.13 = bf16[4,1,256,64]{2,3,1,0:T(8,128)(2,1)} copy(bf16[4,1,256,64]{2,3,1,0:T(8,128)(2,1)} %bitcast.32) | data formatting | bytes 262144
  (2 shorter events, 0.0 us)

commit v2 on v1

--- a/solution.py
+++ b/solution.py
@@ -20,6 +20,8 @@
 GROUPS = 32
 PATCHES = 256
 TILE_PARTS = 8
+LAGS = 8
+UNROLL = 4
 
 
 def times_transposed(x, w):
@@ -27,10 +29,11 @@
 
 
 def kernel(
-    info_ref, scale_ref, end_ref,
+    rows_ref, cols_ref, lags_ref, scales_ref,
     past_ref, tiles_ref, near_ref, inverse_ref, incident_ref,
     out_ref,
-    tiles, near, inverse, incident, gp, acc, slots, pa, pb,
+    tiles, near, inverse, incident, ga, gb, work, acc, slots, pa, pb,
+    order_v, weight_v, order, weight,
     rel1, dir1, s1, rel2, dir2, ts, hist, zr, window, fresh, pre,
     local_sem, g_send, g_recv, d_send, d_recv,
     r_send, r_recv, z_send, z_recv, w_send, w_recv, n_send, n_recv,
@@ -55,8 +58,15 @@
 
     barrier = pltpu.get_barrier_semaphore()
 
-    first = pltpu.make_async_copy(past_ref, gp.at[own], local_sem.at[0])
-    first.start()
+    chunks = ((ga, 0, 6), (gb, 6, 2))
+    firsts = []
+    for c, (held, begin, count) in enumerate(chunks):
+        firsts.append(
+            pltpu.make_async_copy(
+                past_ref.at[pl.ds(begin, count)], held.at[own], local_sem.at[c]
+            )
+        )
+        firsts[c].start()
     loads = []
     part = TILES // TILE_PARTS
     for k in range(TILE_PARTS):
@@ -64,12 +74,12 @@
             pltpu.make_async_copy(
                 tiles_ref.at[pl.ds(k * part, part)],
                 tiles.at[pl.ds(k * part, part)],
-                local_sem.at[4 + k],
+                local_sem.at[8 + k],
             )
         )
-    near_load = pltpu.make_async_copy(near_ref, near, local_sem.at[1])
-    inverse_load = pltpu.make_async_copy(inverse_ref, inverse, local_sem.at[2])
-    incident_load = pltpu.make_async_copy(incident_ref, incident, local_sem.at[3])
+    near_load = pltpu.make_async_copy(near_ref, near, local_sem.at[4])
+    inverse_load = pltpu.make_async_copy(inverse_ref, inverse, local_sem.at[5])
+    incident_load = pltpu.make_async_copy(incident_ref, incident, local_sem.at[6])
 
     partners = [
         {"hist_0": lax.rem(x + 1, 4)},
@@ -89,7 +99,8 @@
     for device in partners:
         pl.semaphore_signal(barrier, inc=1, device_id=device, device_id_type=MESH)
     pl.semaphore_wait(barrier, len(partners))
-    first.wait()
+    for copy in firsts:
+        copy.wait()
 
     def remote(src, dst, send, recv, device):
         return pltpu.make_async_remote_copy(
@@ -102,85 +113,132 @@
     middle = 1 + lax.rem(row, 2)
     outer = 3 * (row // 2)
     blocks = [opposite, 1 + lax.rem(row, 2), 3 - 3 * lax.rem(row, 2)]
-    to_opposite = remote(gp.at[own], gp.at[own], g_send.at[0], g_recv.at[0], {"row": opposite})
-    to_middle = remote(
-        gp.at[own], gp.at[own], g_send.at[1], g_recv.at[2 - inner], {"row": middle}
-    )
-    to_outer = remote(gp.at[own], gp.at[own], g_send.at[2], g_recv.at[1], {"row": outer})
     far = opposite * 2 + cur
-    relayed = remote(gp.at[far], gp.at[far], g_send.at[3], g_recv.at[2], {"row": outer})
-    to_opposite.start()
-    to_middle.start()
-
-    @pl.when(inner == 1)
-    def _():
-        to_outer.start()
-
+    gathers = []
+    for c, (held, begin, count) in enumerate(chunks):
+        mine = held.at[own]
+        theirs = held.at[far]
+        gathers.append((
+            remote(mine, mine, g_send.at[4 * c], g_recv.at[3 * c], {"row": opposite}),
+            remote(mine, mine, g_send.at[4 * c + 1], g_recv.at[3 * c + 2 - inner], {"row": middle}),
+            remote(mine, mine, g_send.at[4 * c + 2], g_recv.at[3 * c + 1], {"row": outer}),
+            remote(theirs, theirs, g_send.at[4 * c + 3], g_recv.at[3 * c + 2], {"row": outer}),
+        ))
     across = []
-    for k, block in enumerate([row] + blocks):
-        spot = gp.at[block * 2 + cur]
-        across.append(remote(spot, spot, d_send.at[k], d_recv.at[k], {"cur": 1 - cur}))
-    across[0].start()
+    for c, (held, begin, count) in enumerate(chunks):
+        moved = []
+        for k, block in enumerate([row] + blocks):
+            spot = held.at[block * 2 + cur]
+            moved.append(
+                remote(spot, spot, d_send.at[4 * c + k], d_recv.at[4 * c + k], {"cur": 1 - cur})
+            )
+        across.append(moved)
+
+    def send_outer(c):
+        @pl.when(inner == 1)
+        def _():
+            gathers[c][2].start()
+
+    gathers[0][0].start()
+    gathers[0][1].start()
+    send_outer(0)
+    for c in range(1, 2):
+        gathers[c][0].start()
+        gathers[c][1].start()
+    for c in range(2):
+        across[c][0].start()
     for load in loads:
         load.start()
     near_load.start()
     inverse_load.start()
     incident_load.start()
 
-    def arrived(k):
-        spot = gp.at[blocks[k] * 2 + cur]
-        remote(spot, spot, g_send.at[k], g_recv.at[k], {"row": opposite}).wait_recv()
-
-    arrived(0)
-
-    @pl.when(inner == 1)
-    def _():
-        relayed.start()
-
-    across[1].start()
+    lane = lax.broadcasted_iota(jnp.int32, (TILES, TILES), 1)
+    line = lax.broadcasted_iota(jnp.int32, (TILES, TILES), 0)
+    nothing = jnp.zeros((TILES, TILES), jnp.int32)
+
+    def turned(value):
+        spread_out = jnp.broadcast_to(value, (TILES, TILES))
+        return jnp.sum(jnp.where(lane == line, spread_out, jnp.zeros_like(spread_out)), axis=1, keepdims=True)
+
+    targets = rows_ref[...]
+    targets_down = turned(targets)
+    ids = lax.broadcasted_iota(jnp.int32, (1, TILES), 1)
+    begins = jnp.minimum(jnp.maximum(LAGS - lags_ref[...], 0), LAGS - STEPS)
+    code = ids + TILES * (cols_ref[...] + 8 * begins)
+    code_down = turned(code)
+    scale_down = turned(scales_ref[...])
+    key = targets * TILES + ids
+    key_down = targets_down * TILES + lax.broadcasted_iota(jnp.int32, (TILES, 1), 0)
+    ahead = jnp.where(jnp.broadcast_to(key, (TILES, TILES)) < key_down, nothing + 1, nothing)
+    rank_down = jnp.sum(ahead, axis=1, keepdims=True)
+    earlier = jnp.where((jnp.broadcast_to(targets, (TILES, TILES)) == targets_down) & (lane < line), nothing + 1, nothing)
+    goes_on = jnp.sum(earlier, axis=1, keepdims=True)
+    goes_on = jnp.where(goes_on > 0, jnp.ones_like(scale_down), jnp.zeros_like(scale_down))
+    here = rank_down == lane
+    zero = jnp.zeros((TILES, TILES), F32)
+    order_v[0:1, 0:TILES] = jnp.sum(jnp.where(here, code_down, nothing), axis=0, keepdims=True)
+    weight_v[0:1, 0:TILES] = jnp.sum(jnp.where(here, scale_down, zero), axis=0, keepdims=True)
+    weight_v[1:2, 0:TILES] = jnp.sum(jnp.where(here, goes_on, zero), axis=0, keepdims=True)
+    upto = jnp.sum(jnp.where(targets_down <= lane, nothing + 1, nothing), axis=0, keepdims=True)
+    order_v[1:2, 0:TILES] = jnp.maximum(upto - 1, 0)
+    order_v[2:3, 0:TILES] = jnp.sum(jnp.where(targets_down == lane, nothing + 1, nothing), axis=0, keepdims=True)
+    order_copy = pltpu.make_async_copy(order_v, order, local_sem.at[7])
+    weight_copy = pltpu.make_async_copy(weight_v, weight, local_sem.at[8 + TILE_PARTS])
+    order_copy.start()
+    weight_copy.start()
+    work[...] = jnp.zeros_like(work)
 
     offsets = (-2, -1, 1, 2)
     window_sends = []
     for k, o in enumerate(offsets):
-        window_sends.append(
-            remote(
-                gp.at[own, pl.ds(5, 3)], window.at[o + 2, pl.ds(0, 3)],
-                w_send.at[k], w_recv.at[k], patch_device(-o),
+        for c, (src, dst) in enumerate((
+            (ga.at[own, pl.ds(5, 1)], window.at[o + 2, pl.ds(0, 1)]),
+            (gb.at[own], window.at[o + 2, pl.ds(1, 2)]),
+        )):
+            window_sends.append(
+                remote(src, dst, w_send.at[2 * k + c], w_recv.at[2 * k + c], patch_device(-o))
             )
-        )
-    arrived(1)
-    across[2].start()
-    arrived(2)
-    across[3].start()
-    for send in window_sends:
-        send.start()
-    window[2, pl.ds(0, 3)] = gp[own, pl.ds(5, 3)]
-    for load in loads:
-        load.wait()
-    for copy in across:
-        copy.wait_recv()
-
-    acc[...] = jnp.zeros_like(acc)
-
-    def one_tile(k, carry):
-        tile = info_ref[0, k]
-        col = info_ref[1, k]
-        begin = info_ref[2, k]
-        held = gp[col, pl.ds(begin, STEPS)].reshape(STEPS * ILLUM, BLOCK)
-        term = times_transposed(held, tiles[tile]) * scale_ref[0, k]
-        total = acc[...] * scale_ref[1, k] + term
-        acc[...] = total
-        slots[k] = total.astype(BF16)
-        return carry
-
-    lax.fori_loop(0, TILES, one_tile, 0, unroll=2)
+
+    def collect(c):
+        held, begin, count = chunks[c]
+        for k, block in enumerate(blocks):
+            spot = held.at[block * 2 + cur]
+            remote(spot, spot, g_send.at[4 * c + k], g_recv.at[3 * c + k], {"row": opposite}).wait_recv()
+            if k == 0:
+                @pl.when(inner == 1)
+                def _():
+                    gathers[c][3].start()
+
+                if c == 0:
+                    for later in range(1, 2):
+                        send_outer(later)
+            across[c][k + 1].start()
+        for copy in across[c]:
+            copy.wait_recv()
+        work[:, pl.ds(begin, count)] = held[...]
+
+    def multiply(t, count, begin_tile=0, end_tile=TILES):
+        def one_tile(k, carry):
+            code = order[0, k]
+            tile = jnp.bitwise_and(code, TILES - 1)
+            col = jnp.bitwise_and(jnp.right_shift(code, 6), 7)
+            begin = jnp.right_shift(code, 9)
+            held = work[col, pl.ds(begin + t, count)].reshape(count * ILLUM, BLOCK)
+            term = times_transposed(held, tiles[tile]) * weight[0, k]
+            total = acc[...] * weight[1, k] + term
+            acc[...] = total
+            slots[k, pl.ds(t, count)] = total.astype(BF16).reshape(count, ILLUM, BLOCK)
+            return carry
+
+        if begin_tile == 0:
+            acc[...] = jnp.zeros_like(acc)
+        lax.fori_loop(begin_tile, end_tile, one_tile, 0, unroll=UNROLL)
 
     def spread(t):
         def one_group(g, carry):
-            end = end_ref[0, g]
-            there = end_ref[1, g]
-            value = slots[end, pl.ds(t * ILLUM, ILLUM)]
-            value = jnp.where(there > 0, value, jnp.zeros_like(value))
+            value = slots[order[1, g], t]
+            value = jnp.where(order[2, g] > 0, value, jnp.zeros_like(value))
             gx = g // 8
             gz = lax.rem(g // 4, 2)
             gy = lax.rem(g, 4)
@@ -222,10 +280,11 @@
 
     state = {}
 
-    def start(t, stage):
+    def start(t, stage, which=(0, 1, 2, 3)):
         for h in (0, 1):
-            state[t, stage, h] = ring(t, stage, h)
-        for n in (0, 1, 2, 3):
+            if 0 in which:
+                state[t, stage, h] = ring(t, stage, h)
+        for n in which:
             for h in (0, 1):
                 state[t, stage, h][0][n].start()
 
@@ -327,101 +386,104 @@
                 if t - 1 + lag < STEPS:
                     pre[t - 1 + lag] = pre[t - 1 + lag] - near_sum(lag, t - 1, everyone)
 
+    collect(0)
+    order_copy.wait()
+    weight_copy.wait()
+    for load in loads:
+        load.wait()
+    window[2, 0] = ga[own, 5]
+    window[2, 1] = gb[own, 0]
+    window[2, 2] = gb[own, 1]
+    multiply(0, 2)
     spread(0)
     start(0, 0)
     spread(1)
-    start(1, 0)
-    spread(2)
-    spread(3)
+    start(1, 0, (0, 1))
+    collect(1)
     relay(0, 0)
-    start(2, 0)
+    start(1, 0, (2, 3))
+    for send in window_sends:
+        send.start()
+    multiply(2, 2, 0, 24)
     relay(1, 0)
+    multiply(2, 2, 24, 40)
     finish_first(0)
     start(0, 1)
-    start(3, 0)
-    start_pre()
-    relay(2, 0)
-    relay(0, 1)
+    multiply(2, 2, 40, 64)
+    spread(2)
+    start(2, 0, (0, 1))
     finish_first(1)
     start(1, 1)
+    relay(0, 1)
+    start(2, 0, (2, 3))
+    spread(3)
+    relay(2, 0)
+    relay(1, 1)
     finish_second(0)
-    relay(3, 0)
-    relay(1, 1)
+    start(3, 0, (0, 1))
+    finish_second(1)
+    start_pre()
     finish_first(2)
     start(2, 1)
+    start(3, 0, (2, 3))
+    relay(3, 0)
+    relay(2, 1)
     near_step(0)
-    finish_second(1)
-    relay(2, 1)
     finish_first(3)
     start(3, 1)
+    finish_second(2)
     near_step(1)
-    finish_second(2)
     relay(3, 1)
+    finish_second(3)
     near_step(2)
-    finish_second(3)
     near_step(3)
 
     for copy in sends:
         copy.wait_send()
     for copy in window_sends:
         copy.wait_send()
-    for copy in across:
-        copy.wait_send()
-    to_opposite.wait_send()
-    to_middle.wait_send()
+    for c in range(2):
+        for copy in across[c]:
+            copy.wait_send()
+        gathers[c][0].wait_send()
+        gathers[c][1].wait_send()
 
     @pl.when(inner == 1)
     def _():
-        to_outer.wait_send()
-        relayed.wait_send()
-
-
-def in_target_order(tile_rows, tile_cols, tile_lags, tile_scales, kept):
-    ids = jnp.arange(TILES, dtype=jnp.int32)
-    key = tile_rows * TILES + ids
-    rank = jnp.sum((key[None, :] < key[:, None]).astype(jnp.int32), axis=1)
-    at = rank[None, :] == ids[:, None]
-
-    def placed(value):
-        return jnp.sum(jnp.where(at, value[None, :], jnp.zeros_like(value)[None, :]), axis=1)
-
-    same = (tile_rows[None, :] == tile_rows[:, None]) & (ids[None, :] < ids[:, None])
-    goes_on = jnp.any(same, axis=1).astype(F32)
-    info = jnp.stack([placed(ids), placed(tile_cols), placed(kept - tile_lags)])
-    scales = jnp.stack([placed(tile_scales), placed(goes_on)])
-    groups = jnp.arange(GROUPS, dtype=jnp.int32)
-    upto = jnp.sum((tile_rows[None, :] <= groups[:, None]).astype(jnp.int32), axis=1)
-    count = jnp.sum((tile_rows[None, :] == groups[:, None]).astype(jnp.int32), axis=1)
-    ends = jnp.stack([jnp.maximum(upto - 1, 0), count])
-    return info, scales, ends
+        for c in range(2):
+            gathers[c][2].wait_send()
+            gathers[c][3].wait_send()
 
 
 def on_device(
     incident, past, hist_tiles, tile_rows, tile_cols, tile_lags, tile_scales, near_tiles, inverses
 ):
     kept = past.shape[1]
-    info, scales, ends = in_target_order(
-        tile_rows[0], tile_cols[0], tile_lags[0], tile_scales[0], kept
-    )
     dma = pltpu.SemaphoreType.DMA
     vmem = pltpu.VMEM
-    smem_spec = pl.BlockSpec(memory_space=pltpu.SMEM)
+    vmem_spec = pl.BlockSpec(memory_space=pltpu.VMEM)
     any_spec = pl.BlockSpec(memory_space=pl.ANY)
     made = pl.pallas_call(
         kernel,
         out_shape=jax.ShapeDtypeStruct((STEPS, ILLUM, BLOCK), BF16),
-        in_specs=[smem_spec] * 3 + [any_spec] * 5,
+        in_specs=[vmem_spec] * 4 + [any_spec] * 5,
         out_specs=pl.BlockSpec(memory_space=pltpu.VMEM),
         scratch_shapes=[
             vmem((TILES, BLOCK, BLOCK), BF16),
             vmem((15, BLOCK, BLOCK), BF16),
             vmem((BLOCK, BLOCK), BF16),
             vmem((STEPS, ILLUM, BLOCK), BF16),
+            vmem((8, 6, ILLUM, BLOCK), BF16),
+            vmem((8, 2, ILLUM, BLOCK), BF16),
             vmem((8, kept, ILLUM, BLOCK), BF16),
-            vmem((STEPS * ILLUM, BLOCK), F32),
-            vmem((TILES, STEPS * ILLUM, BLOCK), BF16),
+            vmem((2 * ILLUM, BLOCK), F32),
+            vmem((TILES, STEPS, ILLUM, BLOCK), BF16),
             vmem((STEPS, 4, 2, 4, HALF, BLOCK), BF16),
             vmem((STEPS, 4, 2, 4, HALF, BLOCK), BF16),
+            vmem((8, 128), jnp.int32),
+            vmem((8, 128), F32),
+            pltpu.SMEM((8, 128), jnp.int32),
+            pltpu.SMEM((8, 128), F32),
             vmem((2, 2, STEPS, 4, HALF, BLOCK), BF16),
             vmem((2, 2, STEPS, 2, 4, HALF, BLOCK), BF16),
             vmem((2, STEPS, 2, 4, HALF, BLOCK), BF16),
@@ -433,16 +495,16 @@
             vmem((5, 6, ILLUM, BLOCK), BF16),
             vmem((3, ILLUM, BLOCK), BF16),
             vmem((STEPS, ILLUM, BLOCK), F32),
-            dma((4 + TILE_PARTS,)),
-            dma((4,)), dma((3,)), dma((4,)), dma((4,)),
+            dma((9 + TILE_PARTS,)),
+            dma((8,)), dma((6,)), dma((8,)), dma((8,)),
             dma((96,)), dma((96,)), dma((4,)), dma((4,)),
-            dma((4,)), dma((4,)), dma((12,)), dma((12,)),
+            dma((8,)), dma((8,)), dma((12,)), dma((12,)),
         ],
         compiler_params=pltpu.CompilerParams(
             collective_id=0, has_side_effects=True, vmem_limit_bytes=58 * 1024 * 1024
         ),
     )(
-        info, scales, ends,
+        tile_rows, tile_cols, tile_lags, tile_scales,
         jnp.swapaxes(past[0], 1, 2),
         hist_tiles[0],
         near_tiles[0].reshape(15, BLOCK, BLOCK),

time: 95.9 us -> 83.6 us (0.87)
  the two profiles are of different devices: /device:TPU:24 before, /device:TPU:1 now
where the time goes in v2:
time: 83.6 us; the launch traced here: 83.5 us
  Pallas kernels  81.9 us (98%)
  local copies, waits for them, and re-layouts  1.57 us (2%)
    pallas_call x1, Pallas kernels, on_device(): pl.pallas_call(kernel, out_shape=jax.ShapeDtypeStruct((STEPS, ILLUM, BLOC...  81.9 us

profile of v2, /device:TPU:1, one launch (start us, length us, event | category | flops | bytes accessed | tf_op | source)
XLA Modules:
  0.0 83.5 jit_solution(4663526084924994429)
XLA Ops:
  0.0 81.9 %shard_map.91 = bf16[4,64,256]{2,1,0:T(8,128)(2,1)} custom-call(s32[1,64]{1,0:T(1,128)} %rows_ref.1, s32[1,64]{1,0:T(1,128)} %cols_ref.1, s32[1,64]{1,0:T(1,128)} %lags_ref.1, f32[1,64]{1,0:T(1,128)} %scales_ref.1, bf16[8,64,256]{2,1,0:T(8,128)(2,1)} %bitcast.17, bf16[64,256,256]{2,1,0:T(8,128)(2,1)} %bitcast.14, bf16[15,256,256]{2,1,0:T(8,128)(2,1)} %bitcast.15, ...), custom_call_target="tpu_custom_call" | custom-call | tf_op jit(solution)/shard_map/pallas_call | solution.py:466
  82.0 1.6 %copy.12 = bf16[4,1,256,64]{2,3,1,0:T(8,128)(2,1)} copy(bf16[4,1,256,64]{2,3,1,0:T(8,128)(2,1)} %bitcast.16) | data formatting | bytes 262144

commit v3 on v2

--- a/solution.py
+++ b/solution.py
@@ -21,7 +21,7 @@
 PATCHES = 256
 TILE_PARTS = 8
 LAGS = 8
-UNROLL = 4
+UNROLL = 8
 
 
 def times_transposed(x, w):
@@ -29,10 +29,11 @@
 
 
 def kernel(
-    rows_ref, cols_ref, lags_ref, scales_ref,
+    rows_hbm, cols_hbm, lags_hbm, scales_hbm,
     past_ref, tiles_ref, near_ref, inverse_ref, incident_ref,
     out_ref,
     tiles, near, inverse, incident, ga, gb, work, acc, slots, pa, pb,
+    rows_ref, cols_ref, lags_ref, scales_ref, small_sem,
     order_v, weight_v, order, weight,
     rel1, dir1, s1, rel2, dir2, ts, hist, zr, window, fresh, pre,
     local_sem, g_send, g_recv, d_send, d_recv,
@@ -67,6 +68,12 @@
             )
         )
         firsts[c].start()
+    smalls = []
+    for k, (src, dst) in enumerate((
+        (rows_hbm, rows_ref), (cols_hbm, cols_ref), (lags_hbm, lags_ref), (scales_hbm, scales_ref),
+    )):
+        smalls.append(pltpu.make_async_copy(src, dst, small_sem.at[k]))
+        smalls[k].start()
     loads = []
     part = TILES // TILE_PARTS
     for k in range(TILE_PARTS):
@@ -161,6 +168,8 @@
         spread_out = jnp.broadcast_to(value, (TILES, TILES))
         return jnp.sum(jnp.where(lane == line, spread_out, jnp.zeros_like(spread_out)), axis=1, keepdims=True)
 
+    for copy in smalls:
+        copy.wait()
     targets = rows_ref[...]
     targets_down = turned(targets)
     ids = lax.broadcasted_iota(jnp.int32, (1, TILES), 1)
@@ -394,6 +403,8 @@
     window[2, 0] = ga[own, 5]
     window[2, 1] = gb[own, 0]
     window[2, 2] = gb[own, 1]
+    for send in window_sends:
+        send.start()
     multiply(0, 2)
     spread(0)
     start(0, 0)
@@ -402,14 +413,12 @@
     collect(1)
     relay(0, 0)
     start(1, 0, (2, 3))
-    for send in window_sends:
-        send.start()
-    multiply(2, 2, 0, 24)
+    multiply(2, 2, 0, 40)
     relay(1, 0)
-    multiply(2, 2, 24, 40)
+    multiply(2, 2, 40, 48)
     finish_first(0)
     start(0, 1)
-    multiply(2, 2, 40, 64)
+    multiply(2, 2, 48, 64)
     spread(2)
     start(2, 0, (0, 1))
     finish_first(1)
@@ -417,25 +426,24 @@
     relay(0, 1)
     start(2, 0, (2, 3))
     spread(3)
+    start_pre()
     relay(2, 0)
+    finish_second(0)
     relay(1, 1)
-    finish_second(0)
-    start(3, 0, (0, 1))
-    finish_second(1)
-    start_pre()
+    start(3, 0)
     finish_first(2)
     start(2, 1)
-    start(3, 0, (2, 3))
+    finish_second(1)
+    near_step(0)
     relay(3, 0)
     relay(2, 1)
-    near_step(0)
+    finish_second(2)
+    near_step(1)
     finish_first(3)
     start(3, 1)
-    finish_second(2)
-    near_step(1)
     relay(3, 1)
+    near_step(2)
     finish_second(3)
-    near_step(2)
     near_step(3)
 
     for copy in sends:
@@ -461,12 +469,11 @@
     kept = past.shape[1]
     dma = pltpu.SemaphoreType.DMA
     vmem = pltpu.VMEM
-    vmem_spec = pl.BlockSpec(memory_space=pltpu.VMEM)
     any_spec = pl.BlockSpec(memory_space=pl.ANY)
     made = pl.pallas_call(
         kernel,
         out_shape=jax.ShapeDtypeStruct((STEPS, ILLUM, BLOCK), BF16),
-        in_specs=[vmem_spec] * 4 + [any_spec] * 5,
+        in_specs=[any_spec] * 9,
         out_specs=pl.BlockSpec(memory_space=pltpu.VMEM),
         scratch_shapes=[
             vmem((TILES, BLOCK, BLOCK), BF16),
@@ -480,6 +487,11 @@
             vmem((TILES, STEPS, ILLUM, BLOCK), BF16),
             vmem((STEPS, 4, 2, 4, HALF, BLOCK), BF16),
             vmem((STEPS, 4, 2, 4, HALF, BLOCK), BF16),
+            vmem((1, TILES), jnp.int32),
+            vmem((1, TILES), jnp.int32),
+            vmem((1, TILES), jnp.int32),
+            vmem((1, TILES), F32),
+            dma((4,)),
             vmem((8, 128), jnp.int32),
             vmem((8, 128), F32),
             pltpu.SMEM((8, 128), jnp.int32),

time: 83.6 us -> 77.9 us (0.932)
  Pallas kernels: 81.9 us -> 76.2 us
    pallas_call x1, Pallas kernels: 81.9 us -> 76.2 us  [on_device(): pl.pallas_call(kernel, out_shape=jax.ShapeDtypeStruct((STEPS, ILLUM, BLOC...]
where the time goes in v3:
time: 77.9 us; the launch traced here: 77.8 us
  Pallas kernels  76.2 us (98%)
  local copies, waits for them, and re-layouts  1.57 us (2%)
    pallas_call x1, Pallas kernels, on_device(): pl.pallas_call(kernel, out_shape=jax.ShapeDtypeStruct((STEPS, ILLUM, BLOC...  76.2 us
    unnamed x1, local copies, waits for them, and re-layouts  1.57 us

profile of v3, /device:TPU:1, one launch (start us, length us, event | category | flops | bytes accessed | tf_op | source)
XLA Modules:
  0.0 77.8 jit_solution(2071278197025451036)
XLA Ops:
  0.0 76.2 %shard_map.91 = bf16[4,64,256]{2,1,0:T(8,128)(2,1)} custom-call(s32[1,64]{1,0:T(1,128)} %rows_hbm.1, s32[1,64]{1,0:T(1,128)} %cols_hbm.1, s32[1,64]{1,0:T(1,128)} %lags_hbm.1, f32[1,64]{1,0:T(1,128)} %scales_hbm.1, bf16[8,64,256]{2,1,0:T(8,128)(2,1)} %bitcast.17, bf16[64,256,256]{2,1,0:T(8,128)(2,1)} %bitcast.14, bf16[15,256,256]{2,1,0:T(8,128)(2,1)} %bitcast.15, ...), custom_call_target="tpu_custom_call" | custom-call | tf_op jit(solution)/shard_map/pallas_call | solution.py:473
  76.2 1.6 %copy.12 = bf16[4,1,256,64]{2,3,1,0:T(8,128)(2,1)} copy(bf16[4,1,256,64]{2,3,1,0:T(8,128)(2,1)} %bitcast.16) | data formatting | bytes 262144

commit v4 on v3

--- a/solution.py
+++ b/solution.py
@@ -359,22 +359,23 @@
         incident_load.wait()
         for send in window_sends:
             send.wait_recv()
-        for t in range(STEPS):
-            total = incident[t].astype(F32)
-            for lag in range(1, 4):
-                if t - lag < 0:
-                    total = total - near_sum(lag, t - lag, everyone)
-            pre[t] = total
+        known_before(0)
+
+    def known_before(t):
+        total = incident[t].astype(F32)
+        for lag in range(1, 4):
+            if t - lag < 0:
+                total = total - near_sum(lag, t - lag, everyone)
+        pre[t] = total
 
     def near_step(t):
-        total = pre[t]
+        pairs[t].wait_recv()
+        total = pre[t] - hist[t] - zr[t].astype(F32)
         if t > 0:
-            for copy in rounds[t - 1]:
-                copy.wait_recv()
-            total = total - near_sum(1, t - 1, offsets)
-        if t == 0 or True:
-            pairs[t].wait_recv()
-        rhs = (total - hist[t] - zr[t].astype(F32)).astype(BF16)
+            for k in (1, 2, 0, 3):
+                rounds[t - 1][k].wait_recv()
+                total = total - near_sum(1, t - 1, (offsets[k],))
+        rhs = total.astype(BF16)
         made = times_transposed(rhs, inverse[...]).astype(BF16)
         out_ref[t] = made
         if t + 1 < STEPS:
@@ -389,6 +390,9 @@
                 rounds[t].append(copy)
                 sends.append(copy)
             window[2, t + 3] = made
+            if t == 0:
+                for later in range(1, STEPS):
+                    known_before(later)
             pre[t + 1] = pre[t + 1] - near_sum(1, t, (0,))
         if t > 0:
             for lag in (2, 3):

time: 77.9 us -> 77.8 us (level)
  no operation moved by 1% of the time
where the time goes in v4:
time: 77.8 us; the launch traced here: 77.7 us
  Pallas kernels  76.1 us (98%)
  local copies, waits for them, and re-layouts  1.57 us (2%)
    pallas_call x1, Pallas kernels, on_device(): pl.pallas_call(kernel, out_shape=jax.ShapeDtypeStruct((STEPS, ILLUM, BLOC...  76.1 us
    unnamed x1, local copies, waits for them, and re-layouts  1.57 us

profile of v4, /device:TPU:1, one launch (start us, length us, event | category | flops | bytes accessed | tf_op | source)
XLA Modules:
  0.0 77.7 jit_solution(2630313927600632778)
XLA Ops:
  0.0 76.1 %shard_map.91 = bf16[4,64,256]{2,1,0:T(8,128)(2,1)} custom-call(s32[1,64]{1,0:T(1,128)} %rows_hbm.1, s32[1,64]{1,0:T(1,128)} %cols_hbm.1, s32[1,64]{1,0:T(1,128)} %lags_hbm.1, f32[1,64]{1,0:T(1,128)} %scales_hbm.1, bf16[8,64,256]{2,1,0:T(8,128)(2,1)} %bitcast.17, bf16[64,256,256]{2,1,0:T(8,128)(2,1)} %bitcast.14, bf16[15,256,256]{2,1,0:T(8,128)(2,1)} %bitcast.15, ...), custom_call_target="tpu_custom_call" | custom-call | tf_op jit(solution)/shard_map/pallas_call | solution.py:477
  76.1 1.6 %copy.12 = bf16[4,1,256,64]{2,3,1,0:T(8,128)(2,1)} copy(bf16[4,1,256,64]{2,3,1,0:T(8,128)(2,1)} %bitcast.16) | data formatting | bytes 262144
